TPU v7x, 256 devices: a whole 4x4x8 slice. The times are simulated.
256 devices in a mesh: arcs: 2 (over z_lo), trow: 8 (over y, core), tcol: 16 (over x, z_hi).
Axes of the slice: x: 4, y: 4, z: 8 (z_hi: 4, z_lo: 2; z = z_hi * 2 + z_lo), core: 2. Of those that a mesh axis runs over, the one named last changes fastest.
Arguments:
- design: bfloat16 [4096, 12288], P(('arcs', 'tcol'), 'trow'), may hold values from -6 to 6
- observed: float32 [4096], P(('arcs', 'tcol')), may hold values from -6 to 6
- arc_counts: int32 [128], P(('arcs', 'tcol')), may hold values from 2 to 32
- arc_weight: float32 [128], P(('arcs', 'tcol')), may hold values from 0.3 to 3
Outputs:
- gram: float32 [12288, 12288], P('trow', ('arcs', 'tcol'))
- rhs: float32 [12288], P('trow')
Inputs may be any that keep to these rules, and one draw needn't show every extreme that they name: `arc_counts`: each arc has at least two valid observations.
All inputs are finite; a program needn't handle non-finite values.
Results may differ from a plain program's by a relative error of at most 0.0055.
Values may be sent and summed in bfloat16 or wider, within the bound.
No kernel may reach another device: no remote copies, remote signals or barrier semaphores. Data moves between devices by JAX's collectives and lax.ppermute only.
A program may use at most 192 MiB of HBM per device.

v0:
```python
import jax
import jax.numpy as jnp
from jax import lax
from jax.sharding import PartitionSpec as P


def from_everyone(x, axis):
    devices = lax.axis_size(axis)
    return lax.all_to_all(jnp.broadcast_to(x[None], (devices, *x.shape)), axis, 0, 0, tiled=True)


def over_copies(x, axis):
    return from_everyone(x, axis).sum(axis=0)


def cut_along(x, dim, devices):
    dims = x.shape
    blocks = x.reshape(*dims[:dim], devices, dims[dim] // devices, *dims[dim + 1 :])
    return jnp.moveaxis(blocks, dim, 0)


def sum_at_owner(x, axis, dim):
    blocks = cut_along(x, dim, lax.axis_size(axis))
    arrived = lax.all_to_all(blocks, axis, split_axis=0, concat_axis=0, tiled=True)
    return arrived.astype(jnp.float32).sum(axis=0)


def fold_with(right, piece):
    return lax.dot_general(
        piece, right, (((0,), (0,)), ((), ())), preferred_element_type=jnp.float32
    )


def local(design, observed, arc_counts, arc_weight):
    row_count, col_width = design.shape
    arc_total = arc_counts.shape[0]
    arc_len = row_count // arc_total
    slot_index = lax.broadcasted_iota(jnp.int32, (arc_total, arc_len), 1)
    valid_mask = (slot_index < arc_counts[:, None]).astype(jnp.float32)
    counts_float = arc_counts.astype(jnp.float32)
    factor = valid_mask * jnp.sqrt(arc_weight)[:, None]
    blocks = design.reshape(arc_total, arc_len, col_width).astype(jnp.float32)
    column_mean = jnp.sum(valid_mask[:, :, None] * blocks, axis=1) / counts_float[:, None]
    centered = (
        (factor[:, :, None] * (blocks - column_mean[:, None, :]))
        .reshape(row_count, col_width)
        .astype(jnp.bfloat16)
    )
    series = observed.reshape(arc_total, arc_len)
    series_mean = jnp.sum(valid_mask * series, axis=1) / counts_float
    weighted = (factor * (series - series_mean[:, None])).reshape(row_count)
    arc_devices = lax.axis_size("arcs")
    tcol_devices = lax.axis_size("tcol")
    obs_total = row_count * arc_devices * tcol_devices
    rhs_part = jnp.dot(weighted, centered.astype(jnp.float32), precision=lax.Precision.HIGHEST)
    rhs = over_copies(rhs_part, ("arcs", "tcol")) * obs_total ** (-0.5)
    every_coef = lax.all_gather(centered, "trow", axis=1, tiled=True)
    full_width = every_coef.shape[1]
    narrow = full_width // (arc_devices * tcol_devices)
    shaped = every_coef.reshape(row_count, arc_devices, tcol_devices, narrow)
    moved = lax.all_to_all(shaped, "tcol", split_axis=2, concat_axis=0, tiled=True)
    right = moved.reshape(row_count * tcol_devices, arc_devices * narrow)
    partial_value = fold_with(right, lax.all_gather(centered, "tcol", axis=0, tiled=True))
    tile = sum_at_owner(partial_value.astype(jnp.bfloat16), "arcs", 1)
    gram = tile * (1.0 / obs_total)
    return (gram, rhs)


def solution(mesh):
    return jax.shard_map(
        local,
        mesh=mesh,
        in_specs=(
            P(("arcs", "tcol"), "trow"),
            P(("arcs", "tcol")),
            P(("arcs", "tcol")),
            P(("arcs", "tcol")),
        ),
        out_specs=(P("trow", ("arcs", "tcol")), P("trow")),
        check_vma=False,
    )
```

profile of v0, /device:TPU:1, one launch (start us, length us, event | category | flops | bytes accessed | tf_op | source)
XLA Modules:
  0.0 264.2 jit_solution(5195800618479505239)
XLA Ops:
  7.2 0.0 all-gather.5.cloned.1.call-start
  7.2 0.7 fusion.4
  7.9 0.7 convert_element_type.33
  8.6 0.7 reshape.101
  9.3 0.7 sqrt.3
  10.0 1.4 select_reduce_fusion
  11.3 0.1 mul.48
  11.4 1.2 multiply_reduce_fusion
  12.6 0.1 broadcast_divide_fusion
  12.7 1.9 fusion.3
  14.6 0.0 all-gather.5.cloned.1.call-update
  14.6 0.0 all-gather.3.cloned.1.call-start
  14.6 0.7 all-gather.3.cloned.1.call-update
  15.3 33.9 %all-gather.5.cloned.1.call-done = bf16[128,12288]{1,0:T(8,128)(2,1)} async-done(((bf16[128,1536]{1,0:T(8,128)(2,1)}), bf16[128,12288]{1,0:T(8,128)(2,1)}) %all-gather.5.cloned.1.call-update) | async-done | bytes 3145744 | tf_op jit(solution)/shard_map/all_gather | solution.py:57
  49.2 3.5 %copy.21 = bf16[128,12288]{0,1:T(8,128)(2,1)S(1)} copy(bf16[128,12288]{1,0:T(8,128)(2,1)} %all-gather.5.cloned.1.call-done) | data formatting | bytes 6291456 | tf_op jit(solution)/shard_map/all_gather | solution.py:57
  52.7 1.9 copy.22
  54.6 0.0 copy-start.2
  54.6 0.0 copy-start
  54.6 0.0 copy-start.1
  54.6 9.4 %all-to-all-start = ((bf16[128,2,16,384]{0,3,1,2:T(8,128)(2,1)}), bf16[128,2,16,384]{0,3,1,2:T(8,128)(2,1)S(1)}, u32[]{:S(2)}, u32[]{:S(2)}) async-start(bf16[128,2,16,384]{0,3,1,2:T(8,128)(2,1)} %copy.22), calls=%async_computation | async-start | bytes 6291456 | tf_op jit(solution)/shard_map/all_to_all | solution.py:61
  64.0 0.0 copy-done.2
  64.0 0.7 convert_divide_fusion
  64.7 0.1 sub.25
  64.7 0.6 sub.26
  65.3 0.0 copy-done
  65.3 0.0 copy-done.1
  65.3 0.9 convolution_reduce_fusion
  66.3 82.1 %all-to-all-done = bf16[128,2,16,384]{0,3,1,2:T(8,128)(2,1)S(1)} async-done(((bf16[128,2,16,384]{0,3,1,2:T(8,128)(2,1)}), bf16[128,2,16,384]{0,3,1,2:T(8,128)(2,1)S(1)}, u32[]{:S(2)}, u32[]{:S(2)}) %all-to-all-start) | async-done | bytes 3145760 | tf_op jit(solution)/shard_map/all_to_all | solution.py:61
  148.4 0.8 broadcast_in_dim.2
  149.2 10.1 %all-to-all-start.2 = ((f32[32,1,1536]{2,1,0:T(1,128)}), f32[32,1,1536]{2,1,0:T(1,128)S(1)}, u32[]{:S(2)}, u32[]{:S(2)}) async-start(f32[32,1,1536]{2,1,0:T(1,128)} %broadcast_in_dim.2), calls=%async_computation.2 | async-start | bytes 393216 | tf_op jit(solution)/shard_map/all_to_all | solution.py:9
  159.2 3.7 %copy.23 = bf16[16,128,2,1,384]{1,0,4,2,3:T(8,128)(2,1)} copy(bf16[16,128,2,1,384]{1,4,2,0,3:T(8,128)(2,1)S(1)} %bitcast.27) | data formatting | bytes 6291456 | tf_op jit(solution)/shard_map/all_to_all | solution.py:61
  163.0 51.0 %all-gather.3.cloned.1.call-done = bf16[2048,1536]{1,0:T(8,128)(2,1)} async-done(((bf16[128,1536]{1,0:T(8,128)(2,1)}), bf16[2048,1536]{1,0:T(8,128)(2,1)}) %all-gather.3.cloned.1.call-update) | async-done | bytes 6291472 | tf_op jit(solution)/shard_map/all_gather | solution.py:63
  213.9 9.5 %convolution_convert_fusion = bf16[1536,768]{0,1:T(8,128)(2,1)} fusion(bf16[2048,1536]{1,0:T(8,128)(2,1)} %all-gather.3.cloned.1.call-done, bf16[96,8,16,128]{3,2,1,0:T(8,128)(2,1)} %bitcast.29), kind=kOutput, calls=%fused_computation.1 | convolution fusion | flops 4833017856 | bytes 11796480 | tf_op jit(solution)/shard_map/dot_general | solution.py:29
  223.4 0.0 all-to-all-done.2
  223.4 3.8 %all-to-all-start.1 = ((bf16[2,1536,384]{1,2,0:T(8,128)(2,1)}), bf16[2,1536,384]{1,2,0:T(8,128)(2,1)S(1)}, u32[]{:S(2)}, u32[]{:S(2)}) async-start(bf16[2,1536,384]{1,2,0:T(8,128)(2,1)} %bitcast.30), calls=%async_computation.1 | async-start | bytes 4718592 | tf_op jit(solution)/shard_map/all_to_all | solution.py:24
  227.3 0.1 reduce_sum.39
  227.4 0.6 broadcast_multiply_fusion.1
  228.0 26.8 %all-to-all-done.1 = bf16[2,1536,384]{1,2,0:T(8,128)(2,1)S(1)} async-done(((bf16[2,1536,384]{1,2,0:T(8,128)(2,1)}), bf16[2,1536,384]{1,2,0:T(8,128)(2,1)S(1)}, u32[]{:S(2)}, u32[]{:S(2)}) %all-to-all-start.1) | async-done | bytes 2359328 | tf_op jit(solution)/shard_map/all_to_all | solution.py:24
  254.8 0.4 convert_reduce_fusion
  255.2 0.2 broadcast_multiply_fusion
  255.4 2.0 copy.25
Async XLA Ops:
  7.2 42.0 %all-gather.5.cloned.1.call-start = ((), (), s32[]{:S(2)}) async-start(), calls=%async_computation.4 | async-start | bytes 3538944 | tf_op jit(solution)/shard_map/all_gather | solution.py:57
  14.6 199.3 %all-gather.3.cloned.1.call-start = ((), (), s32[]{:S(2)}) async-start(), calls=%async_computation.3 | async-start | bytes 6684672 | tf_op jit(solution)/shard_map/all_gather | solution.py:63
  54.6 9.4 %copy-start.2 = (s32[4]{0:T(128)S(1)}, s32[4]{0:T(128)}, u32[]{:S(2)}) copy-start(s32[4]{0:T(128)} %param.6) | copy-start | bytes 52
  54.6 10.7 %copy-start = (bf16[128,1536]{1,0:T(8,128)(2,1)S(1)}, bf16[128,1536]{1,0:T(8,128)(2,1)}, u32[]{:S(2)}) copy-start(bf16[128,1536]{1,0:T(8,128)(2,1)} %fusion.3) | copy-start | bytes 1179652
  54.6 10.7 %copy-start.1 = (f32[128]{0:T(128)S(1)}, f32[128]{0:T(128)}, u32[]{:S(2)}) copy-start(f32[128]{0:T(128)} %param.5) | copy-start | bytes 1540
  54.6 93.8 %all-to-all-start = ((bf16[128,2,16,384]{0,3,1,2:T(8,128)(2,1)}), bf16[128,2,16,384]{0,3,1,2:T(8,128)(2,1)S(1)}, u32[]{:S(2)}, u32[]{:S(2)}) async-start(bf16[128,2,16,384]{0,3,1,2:T(8,128)(2,1)} %copy.22), calls=%async_computation | async-start | bytes 6291456 | tf_op jit(solution)/shard_map/all_to_all | solution.py:61
  149.2 74.3 %all-to-all-start.2 = ((f32[32,1,1536]{2,1,0:T(1,128)}), f32[32,1,1536]{2,1,0:T(1,128)S(1)}, u32[]{:S(2)}, u32[]{:S(2)}) async-start(f32[32,1,1536]{2,1,0:T(1,128)} %broadcast_in_dim.2), calls=%async_computation.2 | async-start | bytes 393216 | tf_op jit(solution)/shard_map/all_to_all | solution.py:9
  223.4 31.3 %all-to-all-start.1 = ((bf16[2,1536,384]{1,2,0:T(8,128)(2,1)}), bf16[2,1536,384]{1,2,0:T(8,128)(2,1)S(1)}, u32[]{:S(2)}, u32[]{:S(2)}) async-start(bf16[2,1536,384]{1,2,0:T(8,128)(2,1)} %bitcast.30), calls=%async_computation.1 | async-start | bytes 4718592 | tf_op jit(solution)/shard_map/all_to_all | solution.py:24
Sparse Core Ops, SparseCore 0:
  14.7 34.4 all-gather.4
  52.2 161.6 all-gather.2
where the time goes:
time: 265 us; the launch traced here: 264 us
  waiting for transfers between devices  194 us (73%)
  starting transfers between devices  23.3 us (9%)
  between operations  14.1 us (5%)
  local copies, waits for them, and re-layouts  14 us (5%)
  matrix products  10.4 us (4%)
  other arithmetic  7.85 us (3%)
    all_to_all x1, waiting for transfers between devices, local(): lax.all_to_all(shaped, 'tcol', split_axis=2, concat_axis=0, tiled=True)  82.1 us
    all_gather x1, waiting for transfers between devices, local(): lax.all_gather(centered, 'tcol', axis=0, tiled=True)  51 us
    all_gather x1, waiting for transfers between devices, local(): every_coef = lax.all_gather(centered, 'trow', axis=1, tiled=True)  33.9 us
    all_to_all x1, waiting for transfers between devices, sum_at_owner(): lax.all_to_all(blocks, axis, split_axis=0, concat_axis=0, tiled=True)  26.8 us
    all_to_all x1, starting transfers between devices, from_everyone(): lax.all_to_all(jnp.broadcast_to(x[None], (devices, *x.shape)), axis, 0, 0...  10.1 us
    dot_general x1, matrix products, fold_with(): lax.dot_general(piece, right, (((0,), (0,)), ((), ())), preferred_element...  9.51 us
    all_to_all x1, starting transfers between devices, local(): lax.all_to_all(shaped, 'tcol', split_axis=2, concat_axis=0, tiled=True)  9.38 us
  transfers between devices with their start and end apart: 5, of which 4 were waited for; matrix products, arithmetic and copies ran while one was open for 8% of the time, Pallas kernels for 0%

commit v1 on v0

--- a/solution.py
+++ b/solution.py
@@ -60,7 +60,12 @@
     shaped = every_coef.reshape(row_count, arc_devices, tcol_devices, narrow)
     moved = lax.all_to_all(shaped, "tcol", split_axis=2, concat_axis=0, tiled=True)
     right = moved.reshape(row_count * tcol_devices, arc_devices * narrow)
-    partial_value = fold_with(right, lax.all_gather(centered, "tcol", axis=0, tiled=True))
+    partial_value = fold_with(
+        right,
+        jnp.concatenate(
+            lax.all_to_all(jnp.stack([centered] * lax.axis_size("tcol")), "tcol", 0, 0), axis=0
+        ),
+    )
     tile = sum_at_owner(partial_value.astype(jnp.bfloat16), "arcs", 1)
     gram = tile * (1.0 / obs_total)
     return (gram, rhs)

time: 265 us -> 345 us (1.30)
  blocking collectives: 0 us -> 82.9 us
  starting transfers between devices: 23.3 us -> 15.2 us
    all_to_all x0 -> x1, blocking collectives: none -> 82.9 us  [local(): lax.all_to_all(shaped, 'tcol', split_axis=2, concat_axis=0, tiled=True)]
    all_to_all x1, waiting for transfers between devices: 82.1 us -> 137 us  [local(): lax.all_to_all(jnp.stack([centered] * lax.axis_size('tcol')), 'tcol', 0, 0)]
    all_gather x1 -> x0, waiting for transfers between devices: 51 us -> none  [local(): lax.all_gather(centered, 'tcol', axis=0, tiled=True)]
    all_to_all x1, starting transfers between devices: 9.38 us -> 4.76 us  [local(): lax.all_to_all(jnp.stack([centered] * lax.axis_size('tcol')), 'tcol', 0, 0)]
  transfers between devices with their start and end apart: 5 -> 4, of which waited for: 4 -> 4; matrix products, arithmetic and copies ran while one was open for 8% -> 5% of each run, Pallas kernels for 0% -> 0%
where the time goes in v1:
time: 345 us; the launch traced here: 342 us
  waiting for transfers between devices  196 us (57%)
  blocking collectives  82.9 us (24%)
  local copies, waits for them, and re-layouts  15.5 us (4%)
  starting transfers between devices  15.2 us (4%)
  between operations  14.1 us (4%)
  matrix products  10.5 us (3%)
  other arithmetic  7.84 us (2%)
    all_to_all x1, waiting for transfers between devices, local(): lax.all_to_all(jnp.stack([centered] * lax.axis_size('tcol')), 'tcol', 0, 0)  137 us
    all_to_all x1, blocking collectives, local(): lax.all_to_all(shaped, 'tcol', split_axis=2, concat_axis=0, tiled=True)  82.9 us
    all_gather x1, waiting for transfers between devices, local(): every_coef = lax.all_gather(centered, 'trow', axis=1, tiled=True)  34.6 us
    all_to_all x1, waiting for transfers between devices, sum_at_owner(): lax.all_to_all(blocks, axis, split_axis=0, concat_axis=0, tiled=True)  24.5 us
    dot_general x1, matrix products, fold_with(): lax.dot_general(piece, right, (((0,), (0,)), ((), ())), preferred_element...  9.53 us
  transfers between devices with their start and end apart: 4, of which 4 were waited for; matrix products, arithmetic and copies ran while one was open for 5% of the time, Pallas kernels for 0%

profile of v1, /device:TPU:1, one launch (start us, length us, event | category | flops | bytes accessed | tf_op | source)
XLA Modules:
  0.0 342.4 jit_solution(2318760989688209803)
XLA Ops:
  7.2 0.0 all-gather.2.cloned.1.call-start
  7.2 0.7 fusion.4
  7.9 0.7 convert_element_type.33
  8.6 0.7 reshape.107
  9.3 0.7 sqrt.3
  10.0 1.4 select_reduce_fusion
  11.3 0.1 mul.48
  11.4 1.2 multiply_reduce_fusion
  12.6 0.1 broadcast_divide_fusion
  12.7 1.9 fusion.3
  14.6 0.0 all-gather.2.cloned.1.call-update
  14.6 34.6 %all-gather.2.cloned.1.call-done = bf16[128,12288]{1,0:T(8,128)(2,1)} async-done(((bf16[128,1536]{1,0:T(8,128)(2,1)}), bf16[128,12288]{1,0:T(8,128)(2,1)}) %all-gather.2.cloned.1.call-update) | async-done | bytes 3145744 | tf_op jit(solution)/shard_map/all_gather | solution.py:57
  49.2 3.5 %copy.22 = bf16[128,12288]{0,1:T(8,128)(2,1)S(1)} copy(bf16[128,12288]{1,0:T(8,128)(2,1)} %all-gather.2.cloned.1.call-done) | data formatting | bytes 6291456 | tf_op jit(solution)/shard_map/all_gather | solution.py:57
  52.7 0.2 copy.23
  52.9 0.0 copy-start
  52.9 82.9 %all_to_all.31 = bf16[128,2,16,384]{0,3,1,2:T(8,128)(2,1)S(1)} all-to-all(bf16[128,2,16,384]{0,3,1,2:T(8,128)(2,1)S(1)} %copy.23), channel_id=1, replica_groups=mesh['arcs'=2,'trow'=8,'tcol'=16] {'tcol'}, dimensions={2} | all-to-all | bytes 6291456 | tf_op jit(solution)/shard_map/all_to_all | solution.py:61
  135.9 0.0 copy-done
  135.9 3.3 stack.2
  139.1 0.0 copy-start.2
  139.1 0.0 copy-start.1
  139.1 4.8 %all-to-all-start = ((bf16[16,128,1536]{2,1,0:T(8,128)(2,1)}), bf16[16,128,1536]{2,1,0:T(8,128)(2,1)}, u32[]{:S(2)}, u32[]{:S(2)}) async-start(bf16[16,128,1536]{2,1,0:T(8,128)(2,1)} %stack.2), calls=%async_computation | async-start | bytes 12582912 | tf_op jit(solution)/shard_map/all_to_all | solution.py:66
  143.9 0.0 copy-done.2
  143.9 0.7 convert_divide_fusion
  144.6 0.1 sub.25
  144.6 0.6 sub.26
  145.2 0.0 copy-done.1
  145.2 0.9 convolution_reduce_fusion
  146.2 3.7 %copy.24 = bf16[16,128,2,1,384]{1,0,4,2,3:T(8,128)(2,1)} copy(bf16[16,128,2,1,384]{1,4,2,0,3:T(8,128)(2,1)S(1)} %bitcast.28) | data formatting | bytes 6291456 | tf_op jit(solution)/shard_map/all_to_all | solution.py:61
  149.9 136.8 %all-to-all-done = bf16[16,128,1536]{2,1,0:T(8,128)(2,1)} async-done(((bf16[16,128,1536]{2,1,0:T(8,128)(2,1)}), bf16[16,128,1536]{2,1,0:T(8,128)(2,1)}, u32[]{:S(2)}, u32[]{:S(2)}) %all-to-all-start) | async-done | bytes 6291488 | tf_op jit(solution)/shard_map/all_to_all | solution.py:66
  286.6 0.8 broadcast_in_dim.2
  287.4 6.6 %all-to-all-start.3 = ((f32[32,1,1536]{2,1,0:T(1,128)}), f32[32,1,1536]{2,1,0:T(1,128)S(1)}, u32[]{:S(2)}, u32[]{:S(2)}) async-start(f32[32,1,1536]{2,1,0:T(1,128)} %broadcast_in_dim.2), calls=%async_computation.3 | async-start | bytes 393216 | tf_op jit(solution)/shard_map/all_to_all | solution.py:9
  294.1 9.5 %convolution_convert_fusion = bf16[1536,768]{0,1:T(8,128)(2,1)} fusion(bf16[2048,1536]{1,0:T(8,128)(2,1)} %bitcast.2, bf16[96,8,16,128]{3,2,1,0:T(8,128)(2,1)} %bitcast.30), kind=kOutput, calls=%fused_computation.1 | convolution fusion | flops 4833017856 | bytes 11796480 | tf_op jit(solution)/shard_map/dot_general | solution.py:29
  303.6 0.3 all-to-all-done.3
  303.9 3.8 %all-to-all-start.2 = ((bf16[2,1536,384]{1,2,0:T(8,128)(2,1)}), bf16[2,1536,384]{1,2,0:T(8,128)(2,1)S(1)}, u32[]{:S(2)}, u32[]{:S(2)}) async-start(bf16[2,1536,384]{1,2,0:T(8,128)(2,1)} %bitcast.31), calls=%async_computation.2 | async-start | bytes 4718592 | tf_op jit(solution)/shard_map/all_to_all | solution.py:24
  307.7 0.1 reduce_sum.39
  307.9 0.6 broadcast_multiply_fusion.1
  308.5 24.5 %all-to-all-done.2 = bf16[2,1536,384]{1,2,0:T(8,128)(2,1)S(1)} async-done(((bf16[2,1536,384]{1,2,0:T(8,128)(2,1)}), bf16[2,1536,384]{1,2,0:T(8,128)(2,1)S(1)}, u32[]{:S(2)}, u32[]{:S(2)}) %all-to-all-start.2) | async-done | bytes 2359328 | tf_op jit(solution)/shard_map/all_to_all | solution.py:24
  333.0 0.4 convert_reduce_fusion
  333.4 0.2 broadcast_multiply_fusion
  333.6 2.0 copy.26
Async XLA Ops:
  7.2 42.0 %all-gather.2.cloned.1.call-start = ((), (), s32[]{:S(2)}) async-start(), calls=%async_computation.4 | async-start | bytes 3538944 | tf_op jit(solution)/shard_map/all_gather | solution.py:57
  52.9 83.0 %copy-start = (bf16[128,1536]{1,0:T(8,128)(2,1)S(1)}, bf16[128,1536]{1,0:T(8,128)(2,1)}, u32[]{:S(2)}) copy-start(bf16[128,1536]{1,0:T(8,128)(2,1)} %fusion.3) | copy-start | bytes 1179652
  139.1 4.8 %copy-start.2 = (s32[4]{0:T(128)S(1)}, s32[4]{0:T(128)}, u32[]{:S(2)}) copy-start(s32[4]{0:T(128)} %param.6) | copy-start | bytes 52
  139.1 6.1 %copy-start.1 = (f32[128]{0:T(128)S(1)}, f32[128]{0:T(128)}, u32[]{:S(2)}) copy-start(f32[128]{0:T(128)} %param.5) | copy-start | bytes 1540
  139.1 147.5 %all-to-all-start = ((bf16[16,128,1536]{2,1,0:T(8,128)(2,1)}), bf16[16,128,1536]{2,1,0:T(8,128)(2,1)}, u32[]{:S(2)}, u32[]{:S(2)}) async-start(bf16[16,128,1536]{2,1,0:T(8,128)(2,1)} %stack.2), calls=%async_computation | async-start | bytes 12582912 | tf_op jit(solution)/shard_map/all_to_all | solution.py:66
  287.4 16.5 %all-to-all-start.3 = ((f32[32,1,1536]{2,1,0:T(1,128)}), f32[32,1,1536]{2,1,0:T(1,128)S(1)}, u32[]{:S(2)}, u32[]{:S(2)}) async-start(f32[32,1,1536]{2,1,0:T(1,128)} %broadcast_in_dim.2), calls=%async_computation.3 | async-start | bytes 393216 | tf_op jit(solution)/shard_map/all_to_all | solution.py:9
  303.9 29.1 %all-to-all-start.2 = ((bf16[2,1536,384]{1,2,0:T(8,128)(2,1)}), bf16[2,1536,384]{1,2,0:T(8,128)(2,1)S(1)}, u32[]{:S(2)}, u32[]{:S(2)}) async-start(bf16[2,1536,384]{1,2,0:T(8,128)(2,1)} %bitcast.31), calls=%async_computation.2 | async-start | bytes 4718592 | tf_op jit(solution)/shard_map/all_to_all | solution.py:24
Sparse Core Ops, SparseCore 0:
  14.7 34.4 all-gather.1
